TPU v7x, 128 devices: a whole 4x4x4 slice. The times are simulated.
128 devices in a mesh: gx: 16 (over y, z), gy: 8 (over x, core).
Axes of the slice: x: 4, y: 4, z: 4, core: 2. Of those that a mesh axis runs over, the one named last changes fastest.
Arguments:
- velocity: float32 [3, 128, 512, 384], P(None, 'gx', 'gy')
- target_profile: float32 [2, 384], replicated, may hold values from 0.5 to 1.5
- disc_turbine: int32 [128, 4], P(('gx', 'gy')), may hold values from -1 to 99, as said below
- disc_start: int32 [3, 128, 4], P(None, ('gx', 'gy')), may hold values from 0 to 256, as said below
- disc_weight: float32 [128, 4, 16, 128], P(('gx', 'gy')), may hold values from 0.2 to 1
- turbine_owner: int32 [100], replicated, may hold values from 0 to 127, as said below
- mode_flag: int32 [100], replicated, may hold values from 0 to 2
- controller_state: float32 [128, 4], P(('gx', 'gy')), may hold values from -4 to 4
Outputs:
- advanced_velocity: float32 [3, 128, 512, 384], P(None, 'gx', 'gy')
- profiles: float32 [4, 384], replicated
- thrust_setpoint: float32 [100], replicated
- controller_next: float32 [128, 4], P(('gx', 'gy'))
Inputs may be any that keep to these rules, and one draw needn't show every extreme that they name: `disc_turbine`: -1 marks an empty slot; every turbine number appears in at least one slot; some device has all 4 slots filled. `disc_start`: row 0 is a cell of the device's block along the first dimension, 0 to 7; row 1 the first of 16 cells along the second, 0 to 48; row 2 the first of 128 heights, 0 to 256. `turbine_owner`: no device owns more than 4 turbines, and some device owns exactly 4.
All inputs are finite; a program needn't handle non-finite values.
Results may differ from a plain program's by a relative error of at most 0.00013.
Values sent between devices are 32-bit elements; how exact they have to be, the bound alone decides.
No kernel may reach another device: no remote copies, remote signals or barrier semaphores. Data moves between devices by JAX's collectives and lax.ppermute only.
A program may use at most 128 MiB of HBM per device.

v0:
```python
import jax
import jax.numpy as jnp
from jax import lax
from jax.sharding import Mesh
from jax.sharding import PartitionSpec as P

STEPS = 4
GX = ("gx_0", "gx_1")
GY = ("gy_0", "gy_1")
GX_GY = ("gx_0", "gx_1", "gy_0", "gy_1")
VISCOSITY = 0.1
TIME_STEP = 0.2
RELAX_TIME = 2.0
CONTROL_STEP = 0.5
GAIN_PROPORTIONAL = 2.0
GAIN_INTEGRAL = 1.0
HIGHEST = lax.Precision.HIGHEST


def by_axis(shard, axes):
    for axis in axes:
        shard = lax.psum(shard, axis)
    return shard


def padded_2(shard, sides, width):
    edges = {}
    for axis, dim in sides:
        size, length = (lax.axis_size(axis), shard.shape[dim])
        up = [(i, (i + 1) % size) for i in range(size)]
        last = lax.slice_in_dim(shard, length - width, length, axis=dim)
        first = lax.slice_in_dim(shard, 0, width, axis=dim)
        edges[dim] = (
            lax.ppermute(last, axis, up),
            lax.ppermute(first, axis, [(b, a) for a, b in up]),
        )
    done = []
    for _, dim in sides:
        low, high = edges[dim]
        around = [(width, width) if d in done else (0, 0) for d in range(shard.ndim)]
        shard = jnp.concatenate([jnp.pad(low, around), shard, jnp.pad(high, around)], axis=dim)
        done.append(dim)
    return shard


def pad_height(block):
    return jnp.pad(block, ((0, 0), (0, 0), (0, 0), (2, 2)))


def tendency(block):
    length_x = block.shape[1] - 4
    length_y = block.shape[2] - 4
    length_z = block.shape[3] - 4

    def shifted(offset_x, offset_y, offset_z):
        return block[
            :,
            2 + offset_x : 2 + offset_x + length_x,
            2 + offset_y : 2 + offset_y + length_y,
            2 + offset_z : 2 + offset_z + length_z,
        ]

    centre = shifted(0, 0, 0)
    grad_x = (
        8.0 * (shifted(1, 0, 0) - shifted(-1, 0, 0)) - (shifted(2, 0, 0) - shifted(-2, 0, 0))
    ) / 12.0
    grad_y = (
        8.0 * (shifted(0, 1, 0) - shifted(0, -1, 0)) - (shifted(0, 2, 0) - shifted(0, -2, 0))
    ) / 12.0
    grad_z = (
        8.0 * (shifted(0, 0, 1) - shifted(0, 0, -1)) - (shifted(0, 0, 2) - shifted(0, 0, -2))
    ) / 12.0
    laplacian = (
        shifted(1, 0, 0)
        + shifted(-1, 0, 0)
        + (shifted(0, 1, 0) + shifted(0, -1, 0))
        + (shifted(0, 0, 1) + shifted(0, 0, -1))
        - 6.0 * centre
    )
    advection = centre[0:1] * grad_x + centre[1:2] * grad_y + centre[2:3] * grad_z
    return VISCOSITY * laplacian - advection


def control_terms(mode_flag):
    rated_speed = jnp.where(mode_flag == 0, 0.7, jnp.where(mode_flag == 1, 0.9, 1.1)).astype(
        jnp.float32
    )
    bias_terms = jnp.where(mode_flag == 0, 1.0, jnp.where(mode_flag == 1, 0.0, -1.0)).astype(
        jnp.float32
    )
    return (rated_speed, bias_terms)


def owner_rank(turbine_owner):
    turbines = turbine_owner.shape[0]
    same_owner = turbine_owner[:, None] == turbine_owner[None, :]
    earlier = (
        jnp.arange(turbines, dtype=jnp.int32)[None, :]
        < jnp.arange(turbines, dtype=jnp.int32)[:, None]
    )
    return jnp.sum((same_owner & earlier).astype(jnp.int32), axis=1)


def thrust_from(bias_terms, speed_error, integral):
    return 0.1 + 0.9 * jax.nn.sigmoid(
        bias_terms - GAIN_PROPORTIONAL * speed_error - GAIN_INTEGRAL * integral
    )


def local(
    velocity,
    target_profile,
    disc_turbine,
    disc_start,
    disc_weight,
    turbine_owner,
    mode_flag,
    controller_state,
):
    blocks_x = lax.axis_size(GX)
    blocks_y = lax.axis_size(GY)
    devices = blocks_x * blocks_y
    device_me = lax.axis_index(GX) * blocks_y + lax.axis_index(GY)
    length_x = velocity.shape[1]
    length_y = velocity.shape[2]
    length_z = velocity.shape[3]
    turbines = mode_flag.shape[0]
    owned = controller_state.shape[1]
    slots = disc_turbine.shape[1]
    tile_y = disc_weight.shape[2]
    tile_z = disc_weight.shape[3]
    weights_local = disc_weight[0]
    start_x = disc_start[0, 0]
    start_y = disc_start[1, 0]
    start_z = disc_start[2, 0]
    turbine_ids = jnp.arange(turbines, dtype=jnp.int32)
    slot_onehot = (disc_turbine[0][:, None] == turbine_ids[None, :]).astype(jnp.float32)
    area_part = jnp.dot(jnp.sum(weights_local, axis=(1, 2)), slot_onehot, precision=HIGHEST)
    disc_area = by_axis(area_part, GX_GY)
    owner_slot = owner_rank(turbine_owner)
    owner_column = turbine_owner * owned + owner_slot
    pick_table = (
        owner_column[:, None] == jnp.arange(devices * owned, dtype=jnp.int32)[None, :]
    ).astype(jnp.float32)
    mine_table = (
        (turbine_owner[:, None] == device_me)
        & (owner_slot[:, None] == jnp.arange(owned, dtype=jnp.int32)[None, :])
    ).astype(jnp.float32)
    live_slot = jnp.sum(mine_table, axis=0)
    rated_speed, bias_terms = control_terms(mode_flag)
    integral = controller_state[0]
    state_all = lax.all_gather(controller_state[0], GX_GY, axis=0, tiled=True)
    integral_all = jnp.dot(pick_table, state_all, precision=HIGHEST)
    plane_cells = float(length_x * blocks_x * length_y * blocks_y)
    profiles = jnp.zeros((4, length_z), jnp.float32)
    thrust = jnp.zeros((turbines,), jnp.float32)
    for turn_index in range(STEPS):
        streamwise = velocity[0]
        contribution = jnp.stack(
            [
                jnp.sum(
                    weights_local[slot_index]
                    * lax.dynamic_slice(
                        streamwise,
                        (start_x[slot_index], start_y[slot_index], start_z[slot_index]),
                        (1, tile_y, tile_z),
                    )[0]
                )
                for slot_index in range(slots)
            ]
        )
        numerator_part = jnp.dot(contribution, slot_onehot, precision=HIGHEST)
        plane_part = jnp.stack(
            [
                jnp.sum(velocity[0], axis=(0, 1)),
                jnp.sum(velocity[1], axis=(0, 1)),
                jnp.sum(velocity[2], axis=(0, 1)),
                jnp.sum(velocity[0] * velocity[2], axis=(0, 1)),
            ]
        )
        plane_sums, numerator = (by_axis(plane_part, GX_GY), by_axis(numerator_part, GX_GY))
        disc_speed = numerator / disc_area
        speed_error = disc_speed - rated_speed
        integral_all = integral_all + CONTROL_STEP * speed_error
        thrust = thrust_from(bias_terms, speed_error, integral_all)
        thrust_factor = 0.5 * thrust * disc_speed * jnp.abs(disc_speed)
        slot_factor = jnp.dot(slot_onehot, thrust_factor, precision=HIGHEST)
        force_field = jnp.zeros((length_x, length_y, length_z), jnp.float32)
        for slot_index in range(slots):
            corner = (start_x[slot_index], start_y[slot_index], start_z[slot_index])
            previous = lax.dynamic_slice(force_field, corner, (1, tile_y, tile_z))
            force_field = lax.dynamic_update_slice(
                force_field,
                previous - slot_factor[slot_index] * weights_local[slot_index][None],
                corner,
            )
        plane_means = plane_sums / plane_cells
        profiles = profiles + jnp.stack(
            [
                plane_means[0],
                plane_means[1],
                plane_means[2],
                plane_means[3] - plane_means[0] * plane_means[2],
            ]
        )
        nudging = (target_profile - plane_means[0:2]) / RELAX_TIME
        padded = padded_2(velocity, ((GX, 1), (GY, 2)), 2)
        changes = tendency(pad_height(padded))
        velocity = jnp.stack(
            [
                velocity[0] + TIME_STEP * (changes[0] + nudging[0][None, None, :] + force_field),
                velocity[1] + TIME_STEP * (changes[1] + nudging[1][None, None, :]),
                velocity[2] + TIME_STEP * changes[2],
            ]
        )
    integral = jnp.dot(integral_all, mine_table, precision=HIGHEST) + (1.0 - live_slot) * integral
    return (velocity, profiles / STEPS, thrust, integral[None, :])


def solution(mesh):
    torus = Mesh(mesh.devices.reshape(4, 4, 4, 2), ("gx_0", "gx_1", "gy_0", "gy_1"))
    placed = (
        P(None, GX, GY, None),
        P(),
        P(GX_GY, None),
        P(None, GX_GY, None),
        P(GX_GY, None, None, None),
        P(),
        P(),
        P(GX_GY, None),
    )
    return jax.shard_map(
        local,
        mesh=torus,
        in_specs=placed,
        out_specs=(P(None, GX, GY, None), P(), P(), P(GX_GY, None)),
        check_vma=False,
    )
```

profile of v0, /device:TPU:1, one launch (start us, length us, event | category | flops | bytes accessed | tf_op | source)
XLA Modules:
  0.0 434.5 jit_solution(4336565369596881345)
XLA Ops:
  7.4 4.6 %collective-permute-start = (f32[3,2,64,384]{3,2,1,0:T(8,128)}, f32[3,2,64,384]{3,2,1,0:T(8,128)}, u32[]{:S(2)}, u32[]{:S(2)}) collective-permute-start(f32[3,2,64,384]{3,2,1,0:T(8,128)} %get-tuple-element.144), channel_id=1, source_target_pairs={{8,0},{16,8},{24,16},{32,24},{40,32},{48,40},{56,48},{64,56},{72,6... | collective-permute-start | bytes 1769480 | tf_op jit(solution)/shard_map/ppermute | solution.py:35
  42.4 6.9 %all-reduce.24 = (f32[4,384]{1,0:T(4,128)S(1)}, f32[100]{0:T(128)S(1)}, f32[100]{0:T(128)S(1)}) all-reduce(f32[4,384]{1,0:T(4,128)S(1)} %pad_maximum_fusion.12, f32[100]{0:T(128)S(1)} %convolution_bitcast_fusion.10, f32[100]{0:T(128)S(1)} %convolution_bitcast_fusion.9), channel_id=1, replica_groups=mesh['gx_0'=4,'gx_1'=4,'gy_0'=4,'gy_1'=2] {'gx_0'}, use_global_device_ids=true, to_apply=%region_4.0 | all-reduce | flops 1736 | bytes 13888 | tf_op jit(solution)/shard_map/psum | solution.py:22
  49.3 7.3 %all-reduce.20 = (f32[4,384]{1,0:T(4,128)S(1)}, f32[100]{0:T(128)S(1)}, f32[100]{0:T(128)S(1)}) all-reduce(f32[4,384]{1,0:T(4,128)S(1)} %get-tuple-element.65, f32[100]{0:T(128)S(1)} %get-tuple-element.66, f32[100]{0:T(128)S(1)} %get-tuple-element.67), channel_id=1, replica_groups=mesh['gx_0'=4,'gx_1'=4,'gy_0'=4,'gy_1'=2] {'gx_1'}, use_global_device_ids=true, to_apply=%region_5.0 | all-reduce | flops 1736 | bytes 13888 | tf_op jit(solution)/shard_map/psum | solution.py:22
  56.6 9.7 %all-reduce.16 = (f32[4,384]{1,0:T(4,128)S(1)}, f32[100]{0:T(128)S(1)}, f32[100]{0:T(128)S(1)}) all-reduce(f32[4,384]{1,0:T(4,128)S(1)} %get-tuple-element.56, f32[100]{0:T(128)S(1)} %get-tuple-element.57, f32[100]{0:T(128)S(1)} %get-tuple-element.58), channel_id=1, replica_groups=mesh['gx_0'=4,'gx_1'=4,'gy_0'=4,'gy_1'=2] {'gy_0'}, use_global_device_ids=true, to_apply=%region_6.0 | all-reduce | flops 1736 | bytes 13888 | tf_op jit(solution)/shard_map/psum | solution.py:22
  66.4 6.2 %all-reduce.28 = (f32[4,384]{1,0:T(4,128)S(1)}, f32[100]{0:T(128)S(1)}, f32[100]{0:T(128)S(1)}) all-reduce(f32[4,384]{1,0:T(4,128)S(1)} %get-tuple-element.47, f32[100]{0:T(128)S(1)} %get-tuple-element.48, f32[100]{0:T(128)S(1)} %get-tuple-element.49), channel_id=1, replica_groups=mesh['gx_0'=4,'gx_1'=4,'gy_0'=4,'gy_1'=2] {'gy_1'}, use_global_device_ids=true, to_apply=%region_7.8 | all-reduce | flops 1736 | bytes 13888 | tf_op jit(solution)/shard_map/psum | solution.py:22
  73.3 62.9 %all-reduce.12 = f32[512]{0:T(512)S(1)} all-reduce(f32[512]{0:T(512)S(1)} %bitcast_dynamic-update-slice_fusion), channel_id=2, replica_groups=mesh['gx_0'=4,'gx_1'=4,'gy_0'=4,'gy_1'=2] {'gx_0','gx_1','gy_0','gy_1'}, use_global_device_ids=true, to_apply=%add.12 | all-reduce | flops 512 | bytes 4096 | tf_op jit(solution)/shard_map/all_gather | solution.py:152
  151.7 8.2 %fusion.33 = f32[3,8,64,384]{3,2,1,0:T(8,128)S(1)} fusion(f32[3,12,68,388]{3,2,1,0:T(8,128)S(1)} %select_maximum_fusion.18, f32[3,12,64,384]{3,2,1,0:T(8,128)} %copy-done.15, f32[3,12,2,384]{3,2,1,0:T(2,128)} %copy-done.31, f32[3,12,2,384]{3,2,1,0:T(2,128)} %copy-done.30, f32[3,10,64,384]{3,2,1,0:T(8,128)} %copy-done.16, ...), kind=kLoop, calls=%fused_computation.81 | loop fusion | flops 17694720 | bytes 29712384 | tf_op jit(solution)/shard_map/sub | solution.py:81
  168.1 7.0 %all-reduce.23 = (f32[4,384]{1,0:T(4,128)S(1)}, f32[100]{0:T(128)S(1)}) all-reduce(f32[4,384]{1,0:T(4,128)S(1)} %pad_maximum_fusion.13, f32[100]{0:T(128)S(1)} %convolution_bitcast_fusion.6), channel_id=1, replica_groups=mesh['gx_0'=4,'gx_1'=4,'gy_0'=4,'gy_1'=2] {'gx_0'}, use_global_device_ids=true, to_apply=%region_26.27 | all-reduce | flops 1636 | bytes 13088 | tf_op jit(solution)/shard_map/psum | solution.py:22
  175.1 7.8 %all-reduce.19 = (f32[4,384]{1,0:T(4,128)S(1)}, f32[100]{0:T(128)S(1)}) all-reduce(f32[4,384]{1,0:T(4,128)S(1)} %get-tuple-element.63, f32[100]{0:T(128)S(1)} %get-tuple-element.64), channel_id=1, replica_groups=mesh['gx_0'=4,'gx_1'=4,'gy_0'=4,'gy_1'=2] {'gx_1'}, use_global_device_ids=true, to_apply=%region_27.28 | all-reduce | flops 1636 | bytes 13088 | tf_op jit(solution)/shard_map/psum | solution.py:22
  182.9 6.5 %all-reduce.15 = (f32[4,384]{1,0:T(4,128)S(1)}, f32[100]{0:T(128)S(1)}) all-reduce(f32[4,384]{1,0:T(4,128)S(1)} %get-tuple-element.54, f32[100]{0:T(128)S(1)} %get-tuple-element.55), channel_id=1, replica_groups=mesh['gx_0'=4,'gx_1'=4,'gy_0'=4,'gy_1'=2] {'gy_0'}, use_global_device_ids=true, to_apply=%region_28.29 | all-reduce | flops 1636 | bytes 13088 | tf_op jit(solution)/shard_map/psum | solution.py:22
  189.4 8.4 %all-reduce.27 = (f32[4,384]{1,0:T(4,128)S(1)}, f32[100]{0:T(128)S(1)}) all-reduce(f32[4,384]{1,0:T(4,128)S(1)} %get-tuple-element.45, f32[100]{0:T(128)S(1)} %get-tuple-element.46), channel_id=1, replica_groups=mesh['gx_0'=4,'gx_1'=4,'gy_0'=4,'gy_1'=2] {'gy_1'}, use_global_device_ids=true, to_apply=%region_29.30 | all-reduce | flops 1636 | bytes 13088 | tf_op jit(solution)/shard_map/psum | solution.py:22
  220.7 7.7 %select_maximum_fusion.12 = f32[3,12,68,388]{3,2,1,0:T(8,128)S(1)} fusion(f32[3,12,2,384]{3,2,1,0:T(2,128)S(1)} %pad.41, f32[3,12,2,384]{3,2,1,0:T(2,128)S(1)} %pad.42, f32[3,2,64,384]{3,2,1,0:T(8,128)} %collective-permute-done.4, f32[3,2,64,384]{3,2,1,0:T(8,128)} %collective-permute-done.5, f32[1,8,64,384]{3,2,1,0:T(8,128)S(1)} %copy-done.11, ...), kind=kLoop, calls=%fused_computation.14 | loop fusion | flops 15197184 | bytes 7559424 | tf_op jit(solution)/shard_map/concatenate | solution.py:41
  228.4 5.5 %pad_maximum_fusion = (f32[3,12,66,384]{3,2,1,0:T(8,128)}, f32[3,12,66,384]{3,2,1,0:T(8,128)}) fusion(f32[3,12,2,384]{3,2,1,0:T(2,128)S(1)} %pad.41, f32[3,2,64,384]{3,2,1,0:T(8,128)} %collective-permute-done.4, f32[1,8,64,384]{3,2,1,0:T(8,128)S(1)} %copy-done.11, f32[1,8,64,384]{3,2,1,0:T(8,128)S(1)} %copy-done.9, f32[1,8,64,384]{3,2,1,0:T(8,128)S(1)} %bitcast.371, ...), kind=kLoop, calls=%fused_computation.27 | loop fusion | flops 9123840 | bytes 11059200 | tf_op jit(solution)/shard_map/concatenate | solution.py:41
  234.0 4.0 pad_maximum_fusion.3
  238.0 9.0 %fusion.24 = f32[3,8,64,384]{3,2,1,0:T(8,128)S(1)} fusion(f32[3,12,68,388]{3,2,1,0:T(8,128)S(1)} %select_maximum_fusion.12, f32[3,12,66,384]{3,2,1,0:T(8,128)} %get-tuple-element.108, f32[3,12,66,384]{3,2,1,0:T(8,128)} %get-tuple-element.107, f32[3,10,64,384]{3,2,1,0:T(8,128)} %get-tuple-element.129, f32[3,10,64,384]{3,2,1,0:T(8,128)} %get-tuple-element.128, ...), kind=kLoop, calls=%fused_computation.69 | loop fusion | flops 16515072 | bytes 35389440 | tf_op jit(solution)/shard_map/sub | solution.py:81
  257.9 7.9 %all-reduce.22 = (f32[4,384]{1,0:T(4,128)S(1)}, f32[100]{0:T(128)S(1)}) all-reduce(f32[4,384]{1,0:T(4,128)S(1)} %pad_maximum_fusion.14, f32[100]{0:T(128)S(1)} %convolution_bitcast_fusion.4), channel_id=1, replica_groups=mesh['gx_0'=4,'gx_1'=4,'gy_0'=4,'gy_1'=2] {'gx_0'}, use_global_device_ids=true, to_apply=%region_42.43 | all-reduce | flops 1636 | bytes 13088 | tf_op jit(solution)/shard_map/psum | solution.py:22
  265.8 8.9 %all-reduce.18 = (f32[4,384]{1,0:T(4,128)S(1)}, f32[100]{0:T(128)S(1)}) all-reduce(f32[4,384]{1,0:T(4,128)S(1)} %get-tuple-element.61, f32[100]{0:T(128)S(1)} %get-tuple-element.62), channel_id=1, replica_groups=mesh['gx_0'=4,'gx_1'=4,'gy_0'=4,'gy_1'=2] {'gx_1'}, use_global_device_ids=true, to_apply=%region_43.44 | all-reduce | flops 1636 | bytes 13088 | tf_op jit(solution)/shard_map/psum | solution.py:22
  274.7 8.1 %all-reduce.14 = (f32[4,384]{1,0:T(4,128)S(1)}, f32[100]{0:T(128)S(1)}) all-reduce(f32[4,384]{1,0:T(4,128)S(1)} %get-tuple-element.52, f32[100]{0:T(128)S(1)} %get-tuple-element.53), channel_id=1, replica_groups=mesh['gx_0'=4,'gx_1'=4,'gy_0'=4,'gy_1'=2] {'gy_0'}, use_global_device_ids=true, to_apply=%region_44.45 | all-reduce | flops 1636 | bytes 13088 | tf_op jit(solution)/shard_map/psum | solution.py:22
  282.9 6.6 %all-reduce.26 = (f32[4,384]{1,0:T(4,128)S(1)}, f32[100]{0:T(128)S(1)}) all-reduce(f32[4,384]{1,0:T(4,128)S(1)} %get-tuple-element.43, f32[100]{0:T(128)S(1)} %get-tuple-element.44), channel_id=1, replica_groups=mesh['gx_0'=4,'gx_1'=4,'gy_0'=4,'gy_1'=2] {'gy_1'}, use_global_device_ids=true, to_apply=%region_45.46 | all-reduce | flops 1636 | bytes 13088 | tf_op jit(solution)/shard_map/psum | solution.py:22
  310.9 7.7 %select_maximum_fusion.6 = f32[3,12,68,388]{3,2,1,0:T(8,128)S(1)} fusion(f32[3,12,2,384]{3,2,1,0:T(2,128)S(1)} %pad.44, f32[3,12,2,384]{3,2,1,0:T(2,128)S(1)} %pad.45, f32[3,2,64,384]{3,2,1,0:T(8,128)S(1)} %collective-permute-done.8, f32[3,2,64,384]{3,2,1,0:T(8,128)} %collective-permute-done.9, f32[1,8,64,384]{3,2,1,0:T(8,128)S(1)} %copy-done.6, ...), kind=kLoop, calls=%fused_computation.8 | loop fusion | flops 15197184 | bytes 7559424 | tf_op jit(solution)/shard_map/concatenate | solution.py:41
  318.6 4.8 %pad_maximum_fusion.1 = (f32[3,12,66,384]{3,2,1,0:T(8,128)}, f32[3,12,66,384]{3,2,1,0:T(8,128)}) fusion(f32[3,12,2,384]{3,2,1,0:T(2,128)S(1)} %pad.44, f32[3,2,64,384]{3,2,1,0:T(8,128)S(1)} %collective-permute-done.8, f32[1,8,64,384]{3,2,1,0:T(8,128)S(1)} %copy-done.6, f32[1,8,64,384]{3,2,1,0:T(8,128)S(1)} %copy-done.4, f32[1,8,64,384]{3,2,1,0:T(8,128)S(1)} %bitcast.366, ...), kind=kLoop, calls=%fused_computation.29 | loop fusion | flops 9123840 | bytes 11059200 | tf_op jit(solution)/shard_map/concatenate | solution.py:41
  323.4 3.0 pad_maximum_fusion.4
  326.4 8.6 %fusion.15 = f32[3,8,64,384]{3,2,1,0:T(8,128)} fusion(f32[3,12,68,388]{3,2,1,0:T(8,128)S(1)} %select_maximum_fusion.6, f32[3,12,66,384]{3,2,1,0:T(8,128)} %get-tuple-element.106, f32[3,12,66,384]{3,2,1,0:T(8,128)} %get-tuple-element.105, f32[3,10,64,384]{3,2,1,0:T(8,128)} %get-tuple-element.121, f32[3,10,64,384]{3,2,1,0:T(8,128)S(1)} %get-tuple-element.120, ...), kind=kLoop, calls=%fused_computation.57 | loop fusion | flops 16515072 | bytes 35389440 | tf_op jit(solution)/shard_map/sub | solution.py:81
  335.0 3.1 multiply_bitcast_fusion.1
  344.0 3.3 collective-permute-start.12
  350.1 14.4 %all-reduce.21 = (f32[4,384]{1,0:T(4,128)S(1)}, f32[100]{0:T(128)S(1)}) all-reduce(f32[4,384]{1,0:T(4,128)S(1)} %pad_maximum_fusion.15, f32[100]{0:T(128)S(1)} %convolution_bitcast_fusion.2), channel_id=1, replica_groups=mesh['gx_0'=4,'gx_1'=4,'gy_0'=4,'gy_1'=2] {'gx_0'}, use_global_device_ids=true, to_apply=%region_58.59 | all-reduce | flops 1636 | bytes 13088 | tf_op jit(solution)/shard_map/psum | solution.py:22
  364.6 7.2 %all-reduce.17 = (f32[4,384]{1,0:T(4,128)S(1)}, f32[100]{0:T(128)S(1)}) all-reduce(f32[4,384]{1,0:T(4,128)S(1)} %get-tuple-element.59, f32[100]{0:T(128)S(1)} %get-tuple-element.60), channel_id=1, replica_groups=mesh['gx_0'=4,'gx_1'=4,'gy_0'=4,'gy_1'=2] {'gx_1'}, use_global_device_ids=true, to_apply=%region_59.60 | all-reduce | flops 1636 | bytes 13088 | tf_op jit(solution)/shard_map/psum | solution.py:22
  371.7 9.7 %all-reduce.13 = (f32[4,384]{1,0:T(4,128)S(1)}, f32[100]{0:T(128)S(1)}) all-reduce(f32[4,384]{1,0:T(4,128)S(1)} %get-tuple-element.50, f32[100]{0:T(128)S(1)} %get-tuple-element.51), channel_id=1, replica_groups=mesh['gx_0'=4,'gx_1'=4,'gy_0'=4,'gy_1'=2] {'gy_0'}, use_global_device_ids=true, to_apply=%region_60.61 | all-reduce | flops 1636 | bytes 13088 | tf_op jit(solution)/shard_map/psum | solution.py:22
  381.4 6.4 %all-reduce.25 = (f32[4,384]{1,0:T(4,128)S(1)}, f32[100]{0:T(128)S(1)}) all-reduce(f32[4,384]{1,0:T(4,128)S(1)} %get-tuple-element.41, f32[100]{0:T(128)S(1)} %get-tuple-element.42), channel_id=1, replica_groups=mesh['gx_0'=4,'gx_1'=4,'gy_0'=4,'gy_1'=2] {'gy_1'}, use_global_device_ids=true, to_apply=%region_61.62 | all-reduce | flops 1636 | bytes 13088 | tf_op jit(solution)/shard_map/psum | solution.py:22
  408.1 7.7 %select_maximum_fusion = f32[3,12,68,388]{3,2,1,0:T(8,128)S(1)} fusion(f32[3,12,2,384]{3,2,1,0:T(2,128)S(1)} %pad.47, f32[3,12,2,384]{3,2,1,0:T(2,128)S(1)} %pad.48, f32[3,2,64,384]{3,2,1,0:T(8,128)S(1)} %collective-permute-done.12, f32[3,2,64,384]{3,2,1,0:T(8,128)} %collective-permute-done.13, f32[1,8,64,384]{3,2,1,0:T(8,128)S(1)} %get-tuple-element.118, ...), kind=kLoop, calls=%fused_computation.2 | loop fusion | flops 15197184 | bytes 7559424 | tf_op jit(solution)/shard_map/concatenate | solution.py:41
  415.8 4.8 %pad_maximum_fusion.2 = (f32[3,12,66,384]{3,2,1,0:T(8,128)}, f32[3,12,66,384]{3,2,1,0:T(8,128)}) fusion(f32[3,12,2,384]{3,2,1,0:T(2,128)S(1)} %pad.47, f32[3,2,64,384]{3,2,1,0:T(8,128)S(1)} %collective-permute-done.12, f32[1,8,64,384]{3,2,1,0:T(8,128)S(1)} %get-tuple-element.118, f32[1,8,64,384]{3,2,1,0:T(8,128)S(1)} %get-tuple-element.81, ...), kind=kLoop, calls=%fused_computation.31 | loop fusion | flops 9123840 | bytes 11059200 | tf_op jit(solution)/shard_map/concatenate | solution.py:41
  422.1 7.5 %fusion.6 = f32[3,8,64,384]{3,2,1,0:T(8,128)} fusion(f32[3,12,68,388]{3,2,1,0:T(8,128)S(1)} %select_maximum_fusion, f32[3,12,66,384]{3,2,1,0:T(8,128)} %get-tuple-element.104, f32[3,12,66,384]{3,2,1,0:T(8,128)} %get-tuple-element.103, f32[3,10,64,384]{3,2,1,0:T(8,128)S(1)} %get-tuple-element.112, f32[3,10,64,384]{3,2,1,0:T(8,128)S(1)} %get-tuple-element.111, ...), kind=kLoop, calls=%fused_computation.45 | loop fusion | flops 16515072 | bytes 35389440 | tf_op jit(solution)/shard_map/sub | solution.py:81
  (299 shorter events, 128.5 us)
Async XLA Ops:
  1.9 143.1 %collective-permute-start.2 = (f32[3,8,2,384]{3,2,1,0:T(2,128)S(1)}, f32[3,8,2,384]{3,2,1,0:T(2,128)S(1)}, u32[]{:S(2)}, u32[]{:S(2)}) collective-permute-start(f32[3,8,2,384]{3,2,1,0:T(2,128)S(1)} %get-tuple-element.143), channel_id=1, source_target_pairs={{1,0},{2,1},{3,2},{4,3},{5,4},{6,5},{7,6},{0,7},{9,8},{10,9},{11,1... | collective-permute-start | bytes 221192 | tf_op jit(solution)/shard_map/ppermute | solution.py:35
  5.6 139.5 %collective-permute-start.1 = (f32[3,2,64,384]{3,2,1,0:T(8,128)}, f32[3,2,64,384]{3,2,1,0:T(8,128)}, u32[]{:S(2)}, u32[]{:S(2)}) collective-permute-start(f32[3,2,64,384]{3,2,1,0:T(8,128)} %get-tuple-element.145), channel_id=1, source_target_pairs={{0,8},{8,16},{16,24},{24,32},{32,40},{40,48},{48,56},{56,64},{64,7... | collective-permute-start | bytes 1769480 | tf_op jit(solution)/shard_map/ppermute | solution.py:34
  7.4 139.9 %collective-permute-start = (f32[3,2,64,384]{3,2,1,0:T(8,128)}, f32[3,2,64,384]{3,2,1,0:T(8,128)}, u32[]{:S(2)}, u32[]{:S(2)}) collective-permute-start(f32[3,2,64,384]{3,2,1,0:T(8,128)} %get-tuple-element.144), channel_id=1, source_target_pairs={{8,0},{16,8},{24,16},{32,24},{40,32},{48,40},{56,48},{64,56},{72,6... | collective-permute-start | bytes 1769480 | tf_op jit(solution)/shard_map/ppermute | solution.py:35
  12.0 133.1 %collective-permute-start.3 = (f32[3,8,2,384]{3,2,1,0:T(2,128)S(1)}, f32[3,8,2,384]{3,2,1,0:T(2,128)S(1)}, u32[]{:S(2)}, u32[]{:S(2)}) collective-permute-start(f32[3,8,2,384]{3,2,1,0:T(2,128)S(1)} %get-tuple-element.142), channel_id=1, source_target_pairs={{0,1},{1,2},{2,3},{3,4},{4,5},{5,6},{6,7},{7,0},{8,9},{9,10},{10,1... | collective-permute-start | bytes 221192 | tf_op jit(solution)/shard_map/ppermute | solution.py:34
  14.8 58.3 %copy-start.34 = (f32[2,384]{1,0:T(2,128)S(1)}, f32[2,384]{1,0:T(2,128)}, u32[]{:S(2)}) copy-start(f32[2,384]{1,0:T(2,128)} %param.9) | copy-start | bytes 9220
  14.8 58.4 %copy-start.57 = (f32[1,4]{1,0:T(1,128)S(1)}, f32[1,4]{1,0:T(1,128)}, u32[]{:S(2)}) copy-start(f32[1,4]{1,0:T(1,128)} %param.15) | copy-start | bytes 52
  14.9 121.3 %copy-start.53 = (s32[100]{0:T(128)S(1)}, s32[100]{0:T(128)}, u32[]{:S(2)}) copy-start(s32[100]{0:T(128)} %param.13) | copy-start | bytes 1204
  14.9 121.5 %copy-start.41 = (s32[100]{0:T(128)S(1)}, s32[100]{0:T(128)}, u32[]{:S(2)}) copy-start(s32[100]{0:T(128)} %param.14) | copy-start | bytes 1204
  72.6 63.8 %copy-start.47 = (f32[100]{0:T(128)}, f32[100]{0:T(128)S(1)}, u32[]{:S(2)}) copy-start(f32[100]{0:T(128)S(1)} %get-tuple-element.76) | copy-start | bytes 1204
  163.2 74.8 %copy-start.1 = (f32[8,64,384]{2,1,0:T(8,128)}, f32[8,64,384]{2,1,0:T(8,128)S(1)}, u32[]{:S(2)}) copy-start(f32[8,64,384]{2,1,0:T(8,128)S(1)} %get-tuple-element.99) | copy-start | bytes 2359300
  197.8 22.3 %collective-permute-start.6 = (f32[3,8,2,384]{3,2,1,0:T(2,128)S(1)}, f32[3,8,2,384]{3,2,1,0:T(2,128)S(1)}, u32[]{:S(2)}, u32[]{:S(2)}) collective-permute-start(f32[3,8,2,384]{3,2,1,0:T(2,128)S(1)} %get-tuple-element.133), channel_id=1, source_target_pairs={{1,0},{2,1},{3,2},{4,3},{5,4},{6,5},{7,6},{0,7},{9,8},{10,9},{11,1... | collective-permute-start | bytes 221192 | tf_op jit(solution)/shard_map/ppermute | solution.py:35
  198.1 22.0 %collective-permute-start.7 = (f32[3,8,2,384]{3,2,1,0:T(2,128)S(1)}, f32[3,8,2,384]{3,2,1,0:T(2,128)S(1)}, u32[]{:S(2)}, u32[]{:S(2)}) collective-permute-start(f32[3,8,2,384]{3,2,1,0:T(2,128)S(1)} %get-tuple-element.132), channel_id=1, source_target_pairs={{0,1},{1,2},{2,3},{3,4},{4,5},{5,6},{6,7},{7,0},{8,9},{9,10},{10,1... | collective-permute-start | bytes 221192 | tf_op jit(solution)/shard_map/ppermute | solution.py:34
  199.6 20.5 %collective-permute-start.4 = (f32[3,2,64,384]{3,2,1,0:T(8,128)}, f32[3,2,64,384]{3,2,1,0:T(8,128)}, u32[]{:S(2)}, u32[]{:S(2)}) collective-permute-start(f32[3,2,64,384]{3,2,1,0:T(8,128)} %get-tuple-element.131), channel_id=1, source_target_pairs={{8,0},{16,8},{24,16},{32,24},{40,32},{48,40},{56,48},{64,56},{72,6... | collective-permute-start | bytes 1769480 | tf_op jit(solution)/shard_map/ppermute | solution.py:35
  200.6 19.5 %collective-permute-start.5 = (f32[3,2,64,384]{3,2,1,0:T(8,128)}, f32[3,2,64,384]{3,2,1,0:T(8,128)}, u32[]{:S(2)}, u32[]{:S(2)}) collective-permute-start(f32[3,2,64,384]{3,2,1,0:T(8,128)} %get-tuple-element.130), channel_id=1, source_target_pairs={{0,8},{8,16},{16,24},{24,32},{32,40},{40,48},{48,56},{56,64},{64,7... | collective-permute-start | bytes 1769480 | tf_op jit(solution)/shard_map/ppermute | solution.py:34
  254.0 38.9 %copy-start.49 = (f32[100]{0:T(128)S(1)}, f32[100]{0:T(128)}, u32[]{:S(2)}) copy-start(f32[100]{0:T(128)} %copy-done.47) | copy-start | bytes 1204
  254.1 56.8 %copy-start.4 = (f32[1,8,64,384]{3,2,1,0:T(8,128)S(1)}, f32[1,8,64,384]{3,2,1,0:T(8,128)}, u32[]{:S(2)}) copy-start(f32[1,8,64,384]{3,2,1,0:T(8,128)} %copy-done.3) | copy-start | bytes 2359300
  254.1 56.8 %copy-start.6 = (f32[1,8,64,384]{3,2,1,0:T(8,128)S(1)}, f32[1,8,64,384]{3,2,1,0:T(8,128)}, u32[]{:S(2)}) copy-start(f32[1,8,64,384]{3,2,1,0:T(8,128)} %copy-done.5) | copy-start | bytes 2359300
  289.5 21.3 %collective-permute-start.10 = (f32[3,8,2,384]{3,2,1,0:T(2,128)S(1)}, f32[3,8,2,384]{3,2,1,0:T(2,128)S(1)}, u32[]{:S(2)}, u32[]{:S(2)}) collective-permute-start(f32[3,8,2,384]{3,2,1,0:T(2,128)S(1)} %get-tuple-element.125), channel_id=1, source_target_pairs={{1,0},{2,1},{3,2},{4,3},{5,4},{6,5},{7,6},{0,7},{9,8},{10,9},{11,1... | collective-permute-start | bytes 221192 | tf_op jit(solution)/shard_map/ppermute | solution.py:35
  289.8 21.0 %collective-permute-start.11 = (f32[3,8,2,384]{3,2,1,0:T(2,128)S(1)}, f32[3,8,2,384]{3,2,1,0:T(2,128)S(1)}, u32[]{:S(2)}, u32[]{:S(2)}) collective-permute-start(f32[3,8,2,384]{3,2,1,0:T(2,128)S(1)} %get-tuple-element.124), channel_id=1, source_target_pairs={{0,1},{1,2},{2,3},{3,4},{4,5},{5,6},{6,7},{7,0},{8,9},{9,10},{10,1... | collective-permute-start | bytes 221192 | tf_op jit(solution)/shard_map/ppermute | solution.py:34
  291.2 19.7 %collective-permute-start.8 = (f32[3,2,64,384]{3,2,1,0:T(8,128)}, f32[3,2,64,384]{3,2,1,0:T(8,128)S(1)}, u32[]{:S(2)}, u32[]{:S(2)}) collective-permute-start(f32[3,2,64,384]{3,2,1,0:T(8,128)} %get-tuple-element.123), channel_id=1, source_target_pairs={{8,0},{16,8},{24,16},{32,24},{40,32},{48,40},{56,48},{64,56},{72,6... | collective-permute-start | bytes 1769480 | tf_op jit(solution)/shard_map/ppermute | solution.py:35
  291.2 19.7 %collective-permute-start.9 = (f32[3,2,64,384]{3,2,1,0:T(8,128)}, f32[3,2,64,384]{3,2,1,0:T(8,128)}, u32[]{:S(2)}, u32[]{:S(2)}) collective-permute-start(f32[3,2,64,384]{3,2,1,0:T(8,128)} %get-tuple-element.122), channel_id=1, source_target_pairs={{0,8},{8,16},{16,24},{24,32},{32,40},{40,48},{48,56},{56,64},{64,7... | collective-permute-start | bytes 1769480 | tf_op jit(solution)/shard_map/ppermute | solution.py:34
  340.3 65.5 %copy-start.58 = (f32[1,4]{1,0:T(1,128)S(1)}, f32[1,4]{1,0:T(1,128)}, u32[]{:S(2)}) copy-start(f32[1,4]{1,0:T(1,128)} %param.15) | copy-start | bytes 52
  340.3 65.5 %copy-start.60 = (s32[100]{0:T(128)S(1)}, s32[100]{0:T(128)}, u32[]{:S(2)}) copy-start(s32[100]{0:T(128)} %copy-done.59) | copy-start | bytes 1204
  340.3 65.5 %copy-start.62 = (pred[100]{0:T(512)(128)(4,1)S(1)}, pred[100]{0:T(512)(128)(4,1)}, u32[]{:S(2)}) copy-start(pred[100]{0:T(512)(128)(4,1)} %copy-done.61) | copy-start | bytes 304
  340.3 65.4 %copy-start.63 = (f32[4]{0:T(128)S(1)}, f32[4]{0:T(128)}, u32[]{:S(2)}) copy-start(f32[4]{0:T(128)} %convert_reduce_fusion.1) | copy-start | bytes 52
  340.4 67.0 %copy-start.33 = (f32[4,384]{1,0:T(4,128)S(1)}, f32[4,384]{1,0:T(4,128)}, u32[]{:S(2)}) copy-start(f32[4,384]{1,0:T(4,128)} %copy-done.32) | copy-start | bytes 18436
  340.4 67.0 %copy-start.39 = (f32[1,384]{1,0:T(1,128)S(1)}, f32[1,384]{1,0:T(1,128)}, u32[]{:S(2)}) copy-start(f32[1,384]{1,0:T(1,128)} %fusion.105) | copy-start | bytes 4612
  340.4 67.0 %copy-start.40 = (f32[1,384]{1,0:T(1,128)S(1)}, f32[1,384]{1,0:T(1,128)}, u32[]{:S(2)}) copy-start(f32[1,384]{1,0:T(1,128)} %fusion.104) | copy-start | bytes 4612
  342.3 65.7 %collective-permute-start.14 = (f32[3,8,2,384]{3,2,1,0:T(2,128)S(1)}, f32[3,8,2,384]{3,2,1,0:T(2,128)S(1)}, u32[]{:S(2)}, u32[]{:S(2)}) collective-permute-start(f32[3,8,2,384]{3,2,1,0:T(2,128)S(1)} %get-tuple-element.116), channel_id=1, source_target_pairs={{1,0},{2,1},{3,2},{4,3},{5,4},{6,5},{7,6},{0,7},{9,8},{10,9},{11,1... | collective-permute-start | bytes 221192 | tf_op jit(solution)/shard_map/ppermute | solution.py:35
  342.4 65.6 %collective-permute-start.15 = (f32[3,8,2,384]{3,2,1,0:T(2,128)S(1)}, f32[3,8,2,384]{3,2,1,0:T(2,128)S(1)}, u32[]{:S(2)}, u32[]{:S(2)}) collective-permute-start(f32[3,8,2,384]{3,2,1,0:T(2,128)S(1)} %get-tuple-element.115), channel_id=1, source_target_pairs={{0,1},{1,2},{2,3},{3,4},{4,5},{5,6},{6,7},{7,0},{8,9},{9,10},{10,1... | collective-permute-start | bytes 221192 | tf_op jit(solution)/shard_map/ppermute | solution.py:34
  344.0 64.1 %collective-permute-start.12 = (f32[3,2,64,384]{3,2,1,0:T(8,128)}, f32[3,2,64,384]{3,2,1,0:T(8,128)S(1)}, u32[]{:S(2)}, u32[]{:S(2)}) collective-permute-start(f32[3,2,64,384]{3,2,1,0:T(8,128)} %get-tuple-element.114), channel_id=1, source_target_pairs={{8,0},{16,8},{24,16},{32,24},{40,32},{48,40},{56,48},{64,56},{72,6... | collective-permute-start | bytes 1769480 | tf_op jit(solution)/shard_map/ppermute | solution.py:35
  347.3 60.8 %collective-permute-start.13 = (f32[3,2,64,384]{3,2,1,0:T(8,128)}, f32[3,2,64,384]{3,2,1,0:T(8,128)}, u32[]{:S(2)}, u32[]{:S(2)}) collective-permute-start(f32[3,2,64,384]{3,2,1,0:T(8,128)} %get-tuple-element.113), channel_id=1, source_target_pairs={{0,8},{8,16},{16,24},{24,32},{32,40},{40,48},{48,56},{56,64},{64,7... | collective-permute-start | bytes 1769480 | tf_op jit(solution)/shard_map/ppermute | solution.py:34
  (48 other events, 553.5 us)
where the time goes:
time: 441 us; the launch traced here: 434 us
  blocking collectives  192 us (44%)
  other arithmetic  126 us (29%)
  local copies, waits for them, and re-layouts  57.6 us (13%)
  between operations  24.7 us (6%)
  starting transfers between devices  21.4 us (5%)
  matrix products  12.6 us (3%)
    psum x16, blocking collectives, by_axis(): shard = lax.psum(shard, axis)  129 us
    all_gather x1, blocking collectives, local(): state_all = lax.all_gather(controller_state[0], GX_GY, axis=0, tiled=True)  62.9 us
    concatenate x10, other arithmetic, padded_2(): jnp.concatenate([jnp.pad(low, around), shard, jnp.pad(high, around)], axi...  49.4 us
    dynamic_update_slice x16, local copies, waits for them, and re-layouts, local(): lax.dynamic_update_slice(force_field, previous - slot_factor[slot_index]...  36.7 us
    sub x4, other arithmetic, tendency(): return VISCOSITY * laplacian - advection  33.3 us
    sub x16, other arithmetic, local(): previous - slot_factor[slot_index] * weights_local[slot_index][None]  17.7 us
    ppermute x8, starting transfers between devices, padded_2(): lax.ppermute(first, axis, [(b, a) for a, b in up])  11.1 us
    dot_general x4, matrix products, local(): numerator_part = jnp.dot(contribution, slot_onehot, precision=HIGHEST)  10.8 us
  transfers between devices with their start and end apart: 16, of which 0 were waited for; matrix products, arithmetic and copies ran while one was open for 18% of the time, Pallas kernels for 0%

commit v1 on v0

--- a/solution.py
+++ b/solution.py
@@ -19,7 +19,7 @@
 
 def by_axis(shard, axes):
     for axis in axes:
-        shard = lax.psum(shard, axis)
+        shard = jnp.sum(lax.all_gather(shard, axis), 0)
     return shard
 
 

time: 441 us -> 620 us (1.41)
  blocking collectives: 192 us -> 358 us
  local copies, waits for them, and re-layouts: 57.6 us -> 67.2 us
    all_gather x0 -> x16, blocking collectives: none -> 161 us  [by_axis(): shard = jnp.sum(lax.all_gather(shard, axis), 0)]
    unnamed x0 -> x16, blocking collectives: none -> 133 us
    psum x16 -> x0, blocking collectives: 129 us -> none  [by_axis(): shard = lax.psum(shard, axis)]
    unnamed x132 -> x190, local copies, waits for them, and re-layouts: 5.62 us -> 12.9 us
  transfers between devices with their start and end apart: 16 -> 16, of which waited for: 0 -> 0; matrix products, arithmetic and copies ran while one was open for 18% -> 15% of each run, Pallas kernels for 0% -> 0%
where the time goes in v1:
time: 620 us; the launch traced here: 612 us
  blocking collectives  358 us (58%)
  other arithmetic  127 us (20%)
  local copies, waits for them, and re-layouts  67.2 us (11%)
  between operations  27.3 us (4%)
  starting transfers between devices  19.7 us (3%)
  matrix products  12.5 us (2%)
    all_gather x16, blocking collectives, by_axis(): shard = jnp.sum(lax.all_gather(shard, axis), 0)  161 us
    unnamed x16, blocking collectives  133 us
    all_gather x1, blocking collectives, local(): state_all = lax.all_gather(controller_state[0], GX_GY, axis=0, tiled=True)  63.1 us
    concatenate x10, other arithmetic, padded_2(): jnp.concatenate([jnp.pad(low, around), shard, jnp.pad(high, around)], axi...  49.4 us
    dynamic_update_slice x16, local copies, waits for them, and re-layouts, local(): lax.dynamic_update_slice(force_field, previous - slot_factor[slot_index]...  36.5 us
    sub x4, other arithmetic, tendency(): return VISCOSITY * laplacian - advection  33.3 us
    sub x16, other arithmetic, local(): previous - slot_factor[slot_index] * weights_local[slot_index][None]  17.6 us
    unnamed x190, local copies, waits for them, and re-layouts  12.9 us
  transfers between devices with their start and end apart: 16, of which 0 were waited for; matrix products, arithmetic and copies ran while one was open for 15% of the time, Pallas kernels for 0%

profile of v1, /device:TPU:1, one launch (start us, length us, event | category | flops | bytes accessed | tf_op | source)
XLA Modules:
  0.0 611.5 jit_solution(14992730794082423227)
XLA Ops:
  31.2 9.1 %all-gather.37 = f32[4,4,384]{2,1,0:T(4,128)S(1)} all-gather(f32[1,4,384]{2,1,0:T(4,128)S(1)} %maximum_bitcast_fusion), channel_id=2, replica_groups=mesh['gx_0'=4,'gx_1'=4,'gy_0'=4,'gy_1'=2] {'gx_0'}, dimensions={0}, use_global_device_ids=true | all-gather | bytes 30720 | tf_op jit(solution)/shard_map/all_gather | solution.py:22
  40.3 9.1 %all-gather.38 = f32[4,4,384]{2,1,0:T(4,128)S(1)} all-gather(f32[1,4,384]{2,1,0:T(4,128)S(1)} %bitcast.406), channel_id=3, replica_groups=mesh['gx_0'=4,'gx_1'=4,'gy_0'=4,'gy_1'=2] {'gx_1'}, dimensions={0}, use_global_device_ids=true | all-gather | bytes 30720 | tf_op jit(solution)/shard_map/all_gather | solution.py:22
  49.4 10.0 %all-gather.39 = f32[4,4,384]{2,1,0:T(4,128)S(1)} all-gather(f32[1,4,384]{2,1,0:T(4,128)S(1)} %bitcast.407), channel_id=4, replica_groups=mesh['gx_0'=4,'gx_1'=4,'gy_0'=4,'gy_1'=2] {'gy_0'}, dimensions={0}, use_global_device_ids=true | all-gather | bytes 30720 | tf_op jit(solution)/shard_map/all_gather | solution.py:22
  59.5 10.2 %all-gather.40 = f32[2,4,384]{2,1,0:T(4,128)S(1)} all-gather(f32[1,4,384]{2,1,0:T(4,128)S(1)} %bitcast.402), channel_id=5, replica_groups=mesh['gx_0'=4,'gx_1'=4,'gy_0'=4,'gy_1'=2] {'gy_1'}, dimensions={0}, use_global_device_ids=true | all-gather | bytes 18432 | tf_op jit(solution)/shard_map/all_gather | solution.py:22
  91.6 7.6 %all-reduce.34 = (f32[400]{0:T(512)S(1)}, f32[400]{0:T(512)S(1)}) all-reduce(f32[400]{0:T(512)S(1)} %dynamic-update-slice.1, f32[400]{0:T(512)S(1)} %dynamic-update-slice.5), channel_id=7, replica_groups=mesh['gx_0'=4,'gx_1'=4,'gy_0'=4,'gy_1'=2] {'gx_1'}, use_global_device_ids=true, to_apply=%add.13 | all-reduce | flops 800 | bytes 6400
  109.5 8.5 %all-reduce.36 = (f32[200]{0:T(256)S(1)}, f32[200]{0:T(256)S(1)}) all-reduce(f32[200]{0:T(256)S(1)} %dynamic-update-slice.3, f32[200]{0:T(256)S(1)} %dynamic-update-slice.7), channel_id=9, replica_groups=mesh['gx_0'=4,'gx_1'=4,'gy_0'=4,'gy_1'=2] {'gy_1'}, use_global_device_ids=true, to_apply=%add.15 | all-reduce | flops 400 | bytes 3200
  118.2 63.1 %all-reduce.20 = f32[512]{0:T(512)S(1)} all-reduce(f32[512]{0:T(512)S(1)} %bitcast_dynamic-update-slice_fusion), channel_id=14, replica_groups=mesh['gx_0'=4,'gx_1'=4,'gy_0'=4,'gy_1'=2] {'gx_0','gx_1','gy_0','gy_1'}, use_global_device_ids=true, to_apply=%add.20 | all-reduce | flops 512 | bytes 4096 | tf_op jit(solution)/shard_map/all_gather | solution.py:152
  197.7 8.2 %fusion.33 = f32[3,8,64,384]{3,2,1,0:T(8,128)S(1)} fusion(f32[3,12,68,388]{3,2,1,0:T(8,128)S(1)} %select_maximum_fusion.18, f32[3,12,64,384]{3,2,1,0:T(8,128)} %copy-done.15, f32[3,12,2,384]{3,2,1,0:T(2,128)} %copy-done.31, f32[3,12,2,384]{3,2,1,0:T(2,128)} %copy-done.30, f32[3,10,64,384]{3,2,1,0:T(8,128)} %copy-done.16, ...), kind=kLoop, calls=%fused_computation.81 | loop fusion | flops 17694720 | bytes 29712384 | tf_op jit(solution)/shard_map/sub | solution.py:81
  211.4 9.1 %all-gather.41 = f32[4,4,384]{2,1,0:T(4,128)S(1)} all-gather(f32[1,4,384]{2,1,0:T(4,128)S(1)} %maximum_bitcast_fusion.1), channel_id=15, replica_groups=mesh['gx_0'=4,'gx_1'=4,'gy_0'=4,'gy_1'=2] {'gx_0'}, dimensions={0}, use_global_device_ids=true | all-gather | bytes 30720 | tf_op jit(solution)/shard_map/all_gather | solution.py:22
  220.5 9.1 %all-gather.42 = f32[4,4,384]{2,1,0:T(4,128)S(1)} all-gather(f32[1,4,384]{2,1,0:T(4,128)S(1)} %bitcast.408), channel_id=16, replica_groups=mesh['gx_0'=4,'gx_1'=4,'gy_0'=4,'gy_1'=2] {'gx_1'}, dimensions={0}, use_global_device_ids=true | all-gather | bytes 30720 | tf_op jit(solution)/shard_map/all_gather | solution.py:22
  229.6 9.1 %all-gather.43 = f32[4,4,384]{2,1,0:T(4,128)S(1)} all-gather(f32[1,4,384]{2,1,0:T(4,128)S(1)} %bitcast.409), channel_id=17, replica_groups=mesh['gx_0'=4,'gx_1'=4,'gy_0'=4,'gy_1'=2] {'gy_0'}, dimensions={0}, use_global_device_ids=true | all-gather | bytes 30720 | tf_op jit(solution)/shard_map/all_gather | solution.py:22
  238.7 10.9 %all-gather.44 = f32[2,4,384]{2,1,0:T(4,128)S(1)} all-gather(f32[1,4,384]{2,1,0:T(4,128)S(1)} %bitcast.403), channel_id=18, replica_groups=mesh['gx_0'=4,'gx_1'=4,'gy_0'=4,'gy_1'=2] {'gy_1'}, dimensions={0}, use_global_device_ids=true | all-gather | bytes 18432 | tf_op jit(solution)/shard_map/all_gather | solution.py:22
  256.5 15.2 %all-reduce.21 = f32[400]{0:T(512)S(1)} all-reduce(f32[400]{0:T(512)S(1)} %dynamic-update-slice.9), channel_id=19, replica_groups=mesh['gx_0'=4,'gx_1'=4,'gy_0'=4,'gy_1'=2] {'gx_0'}, use_global_device_ids=true, to_apply=%add.21 | all-reduce | flops 400 | bytes 3200
  272.0 7.7 %all-reduce.22 = f32[400]{0:T(512)S(1)} all-reduce(f32[400]{0:T(512)S(1)} %dynamic-update-slice.10), channel_id=20, replica_groups=mesh['gx_0'=4,'gx_1'=4,'gy_0'=4,'gy_1'=2] {'gx_1'}, use_global_device_ids=true, to_apply=%add.22 | all-reduce | flops 400 | bytes 3200
  313.8 7.7 %select_maximum_fusion.12 = f32[3,12,68,388]{3,2,1,0:T(8,128)S(1)} fusion(f32[3,12,2,384]{3,2,1,0:T(2,128)S(1)} %pad.41, f32[3,12,2,384]{3,2,1,0:T(2,128)S(1)} %pad.42, f32[3,2,64,384]{3,2,1,0:T(8,128)} %collective-permute-done.4, f32[3,2,64,384]{3,2,1,0:T(8,128)} %collective-permute-done.5, f32[1,8,64,384]{3,2,1,0:T(8,128)S(1)} %copy-done.11, ...), kind=kLoop, calls=%fused_computation.14 | loop fusion | flops 15197184 | bytes 7559424 | tf_op jit(solution)/shard_map/concatenate | solution.py:41
  331.1 9.0 %fusion.24 = f32[3,8,64,384]{3,2,1,0:T(8,128)S(1)} fusion(f32[3,12,68,388]{3,2,1,0:T(8,128)S(1)} %select_maximum_fusion.12, f32[3,12,66,384]{3,2,1,0:T(8,128)} %get-tuple-element.80, f32[3,12,66,384]{3,2,1,0:T(8,128)} %get-tuple-element.79, f32[3,10,64,384]{3,2,1,0:T(8,128)} %get-tuple-element.101, f32[3,10,64,384]{3,2,1,0:T(8,128)} %get-tuple-element.100, ...), kind=kLoop, calls=%fused_computation.69 | loop fusion | flops 16515072 | bytes 35389440 | tf_op jit(solution)/shard_map/sub | solution.py:81
  348.4 9.3 %all-gather.45 = f32[4,4,384]{2,1,0:T(4,128)S(1)} all-gather(f32[1,4,384]{2,1,0:T(4,128)S(1)} %maximum_bitcast_fusion.2), channel_id=23, replica_groups=mesh['gx_0'=4,'gx_1'=4,'gy_0'=4,'gy_1'=2] {'gx_0'}, dimensions={0}, use_global_device_ids=true | all-gather | bytes 30720 | tf_op jit(solution)/shard_map/all_gather | solution.py:22
  357.8 9.1 %all-gather.46 = f32[4,4,384]{2,1,0:T(4,128)S(1)} all-gather(f32[1,4,384]{2,1,0:T(4,128)S(1)} %bitcast.410), channel_id=24, replica_groups=mesh['gx_0'=4,'gx_1'=4,'gy_0'=4,'gy_1'=2] {'gx_1'}, dimensions={0}, use_global_device_ids=true | all-gather | bytes 30720 | tf_op jit(solution)/shard_map/all_gather | solution.py:22
  366.8 9.1 %all-gather.47 = f32[4,4,384]{2,1,0:T(4,128)S(1)} all-gather(f32[1,4,384]{2,1,0:T(4,128)S(1)} %bitcast.411), channel_id=25, replica_groups=mesh['gx_0'=4,'gx_1'=4,'gy_0'=4,'gy_1'=2] {'gy_0'}, dimensions={0}, use_global_device_ids=true | all-gather | bytes 30720 | tf_op jit(solution)/shard_map/all_gather | solution.py:22
  375.9 10.2 %all-gather.48 = f32[2,4,384]{2,1,0:T(4,128)S(1)} all-gather(f32[1,4,384]{2,1,0:T(4,128)S(1)} %bitcast.404), channel_id=26, replica_groups=mesh['gx_0'=4,'gx_1'=4,'gy_0'=4,'gy_1'=2] {'gy_1'}, dimensions={0}, use_global_device_ids=true | all-gather | bytes 18432 | tf_op jit(solution)/shard_map/all_gather | solution.py:22
  392.3 15.2 %all-reduce.25 = f32[400]{0:T(512)S(1)} all-reduce(f32[400]{0:T(512)S(1)} %dynamic-update-slice.13), channel_id=27, replica_groups=mesh['gx_0'=4,'gx_1'=4,'gy_0'=4,'gy_1'=2] {'gx_0'}, use_global_device_ids=true, to_apply=%add.25 | all-reduce | flops 400 | bytes 3200
  407.9 7.9 %all-reduce.26 = f32[400]{0:T(512)S(1)} all-reduce(f32[400]{0:T(512)S(1)} %dynamic-update-slice.14), channel_id=28, replica_groups=mesh['gx_0'=4,'gx_1'=4,'gy_0'=4,'gy_1'=2] {'gx_1'}, use_global_device_ids=true, to_apply=%add.26 | all-reduce | flops 400 | bytes 3200
  448.0 7.7 %select_maximum_fusion.6 = f32[3,12,68,388]{3,2,1,0:T(8,128)S(1)} fusion(f32[3,12,2,384]{3,2,1,0:T(2,128)S(1)} %pad.44, f32[3,12,2,384]{3,2,1,0:T(2,128)S(1)} %pad.45, f32[3,2,64,384]{3,2,1,0:T(8,128)S(1)} %collective-permute-done.8, f32[3,2,64,384]{3,2,1,0:T(8,128)} %collective-permute-done.9, f32[1,8,64,384]{3,2,1,0:T(8,128)S(1)} %copy-done.6, ...), kind=kLoop, calls=%fused_computation.8 | loop fusion | flops 15197184 | bytes 7559424 | tf_op jit(solution)/shard_map/concatenate | solution.py:41
  463.5 8.6 %fusion.15 = f32[3,8,64,384]{3,2,1,0:T(8,128)} fusion(f32[3,12,68,388]{3,2,1,0:T(8,128)S(1)} %select_maximum_fusion.6, f32[3,12,66,384]{3,2,1,0:T(8,128)} %get-tuple-element.78, f32[3,12,66,384]{3,2,1,0:T(8,128)} %get-tuple-element.77, f32[3,10,64,384]{3,2,1,0:T(8,128)} %get-tuple-element.93, f32[3,10,64,384]{3,2,1,0:T(8,128)S(1)} %get-tuple-element.92, ...), kind=kLoop, calls=%fused_computation.57 | loop fusion | flops 16515072 | bytes 35389440 | tf_op jit(solution)/shard_map/sub | solution.py:81
  482.6 19.2 %all-gather.49 = f32[4,4,384]{2,1,0:T(4,128)S(1)} all-gather(f32[1,4,384]{2,1,0:T(4,128)S(1)} %maximum_bitcast_fusion.3), channel_id=31, replica_groups=mesh['gx_0'=4,'gx_1'=4,'gy_0'=4,'gy_1'=2] {'gx_0'}, dimensions={0}, use_global_device_ids=true | all-gather | bytes 30720 | tf_op jit(solution)/shard_map/all_gather | solution.py:22
  501.8 9.1 %all-gather.50 = f32[4,4,384]{2,1,0:T(4,128)S(1)} all-gather(f32[1,4,384]{2,1,0:T(4,128)S(1)} %bitcast.412), channel_id=32, replica_groups=mesh['gx_0'=4,'gx_1'=4,'gy_0'=4,'gy_1'=2] {'gx_1'}, dimensions={0}, use_global_device_ids=true | all-gather | bytes 30720 | tf_op jit(solution)/shard_map/all_gather | solution.py:22
  510.9 9.1 %all-gather.51 = f32[4,4,384]{2,1,0:T(4,128)S(1)} all-gather(f32[1,4,384]{2,1,0:T(4,128)S(1)} %bitcast.413), channel_id=33, replica_groups=mesh['gx_0'=4,'gx_1'=4,'gy_0'=4,'gy_1'=2] {'gy_0'}, dimensions={0}, use_global_device_ids=true | all-gather | bytes 30720 | tf_op jit(solution)/shard_map/all_gather | solution.py:22
  519.9 9.8 %all-gather.52 = f32[2,4,384]{2,1,0:T(4,128)S(1)} all-gather(f32[1,4,384]{2,1,0:T(4,128)S(1)} %bitcast.405), channel_id=34, replica_groups=mesh['gx_0'=4,'gx_1'=4,'gy_0'=4,'gy_1'=2] {'gy_1'}, dimensions={0}, use_global_device_ids=true | all-gather | bytes 18432 | tf_op jit(solution)/shard_map/all_gather | solution.py:22
  539.9 8.9 %all-reduce.30 = f32[400]{0:T(512)S(1)} all-reduce(f32[400]{0:T(512)S(1)} %dynamic-update-slice.18), channel_id=36, replica_groups=mesh['gx_0'=4,'gx_1'=4,'gy_0'=4,'gy_1'=2] {'gx_1'}, use_global_device_ids=true, to_apply=%add.30 | all-reduce | flops 400 | bytes 3200
  556.0 8.8 %all-reduce.32 = f32[200]{0:T(256)S(1)} all-reduce(f32[200]{0:T(256)S(1)} %dynamic-update-slice.20), channel_id=38, replica_groups=mesh['gx_0'=4,'gx_1'=4,'gy_0'=4,'gy_1'=2] {'gy_1'}, use_global_device_ids=true, to_apply=%add.32 | all-reduce | flops 200 | bytes 1600
  585.1 7.7 %select_maximum_fusion = f32[3,12,68,388]{3,2,1,0:T(8,128)S(1)} fusion(f32[3,12,2,384]{3,2,1,0:T(2,128)S(1)} %pad.47, f32[3,12,2,384]{3,2,1,0:T(2,128)S(1)} %pad.48, f32[3,2,64,384]{3,2,1,0:T(8,128)S(1)} %collective-permute-done.12, f32[3,2,64,384]{3,2,1,0:T(8,128)} %collective-permute-done.13, f32[1,8,64,384]{3,2,1,0:T(8,128)S(1)} %get-tuple-element.90, ...), kind=kLoop, calls=%fused_computation.2 | loop fusion | flops 15197184 | bytes 7559424 | tf_op jit(solution)/shard_map/concatenate | solution.py:41
  599.1 7.5 %fusion.6 = f32[3,8,64,384]{3,2,1,0:T(8,128)} fusion(f32[3,12,68,388]{3,2,1,0:T(8,128)S(1)} %select_maximum_fusion, f32[3,12,66,384]{3,2,1,0:T(8,128)} %get-tuple-element.76, f32[3,12,66,384]{3,2,1,0:T(8,128)} %get-tuple-element.75, f32[3,10,64,384]{3,2,1,0:T(8,128)S(1)} %get-tuple-element.84, f32[3,10,64,384]{3,2,1,0:T(8,128)S(1)} %get-tuple-element.83, ...), kind=kLoop, calls=%fused_computation.45 | loop fusion | flops 16515072 | bytes 35389440 | tf_op jit(solution)/shard_map/sub | solution.py:81
  (428 shorter events, 223.6 us)
Async XLA Ops:
  1.9 189.1 %collective-permute-start.2 = (f32[3,8,2,384]{3,2,1,0:T(2,128)S(1)}, f32[3,8,2,384]{3,2,1,0:T(2,128)S(1)}, u32[]{:S(2)}, u32[]{:S(2)}) collective-permute-start(f32[3,8,2,384]{3,2,1,0:T(2,128)S(1)} %get-tuple-element.115), channel_id=1, source_target_pairs={{1,0},{2,1},{3,2},{4,3},{5,4},{6,5},{7,6},{0,7},{9,8},{10,9},{11,1... | collective-permute-start | bytes 221192 | tf_op jit(solution)/shard_map/ppermute | solution.py:35
  5.6 185.5 %collective-permute-start.1 = (f32[3,2,64,384]{3,2,1,0:T(8,128)}, f32[3,2,64,384]{3,2,1,0:T(8,128)}, u32[]{:S(2)}, u32[]{:S(2)}) collective-permute-start(f32[3,2,64,384]{3,2,1,0:T(8,128)} %get-tuple-element.117), channel_id=1, source_target_pairs={{0,8},{8,16},{16,24},{24,32},{32,40},{40,48},{48,56},{56,64},{64,7... | collective-permute-start | bytes 1769480 | tf_op jit(solution)/shard_map/ppermute | solution.py:34
  7.4 185.9 %collective-permute-start = (f32[3,2,64,384]{3,2,1,0:T(8,128)}, f32[3,2,64,384]{3,2,1,0:T(8,128)}, u32[]{:S(2)}, u32[]{:S(2)}) collective-permute-start(f32[3,2,64,384]{3,2,1,0:T(8,128)} %get-tuple-element.116), channel_id=1, source_target_pairs={{8,0},{16,8},{24,16},{32,24},{40,32},{48,40},{56,48},{64,56},{72,6... | collective-permute-start | bytes 1769480 | tf_op jit(solution)/shard_map/ppermute | solution.py:35
  12.0 179.1 %collective-permute-start.3 = (f32[3,8,2,384]{3,2,1,0:T(2,128)S(1)}, f32[3,8,2,384]{3,2,1,0:T(2,128)S(1)}, u32[]{:S(2)}, u32[]{:S(2)}) collective-permute-start(f32[3,8,2,384]{3,2,1,0:T(2,128)S(1)} %get-tuple-element.114), channel_id=1, source_target_pairs={{0,1},{1,2},{2,3},{3,4},{4,5},{5,6},{6,7},{7,0},{8,9},{9,10},{10,1... | collective-permute-start | bytes 221192 | tf_op jit(solution)/shard_map/ppermute | solution.py:34
  14.9 92.8 %copy-start.67 = (u32[128]{0:T(128)S(1)}, u32[128]{0:T(128)}, u32[]{:S(2)}) copy-start(u32[128]{0:T(128)} %constant.140) | copy-start | bytes 1540
  14.9 103.2 %copy-start.60 = (f32[1,4]{1,0:T(1,128)S(1)}, f32[1,4]{1,0:T(1,128)}, u32[]{:S(2)}) copy-start(f32[1,4]{1,0:T(1,128)} %param.15) | copy-start | bytes 52
  14.9 166.4 %copy-start.56 = (s32[100]{0:T(128)S(1)}, s32[100]{0:T(128)}, u32[]{:S(2)}) copy-start(s32[100]{0:T(128)} %param.13) | copy-start | bytes 1204
  14.9 167.1 %copy-start.47 = (s32[100]{0:T(128)S(1)}, s32[100]{0:T(128)}, u32[]{:S(2)}) copy-start(s32[100]{0:T(128)} %param.14) | copy-start | bytes 1204
  209.2 121.9 %copy-start.1 = (f32[8,64,384]{2,1,0:T(8,128)}, f32[8,64,384]{2,1,0:T(8,128)S(1)}, u32[]{:S(2)}) copy-start(f32[8,64,384]{2,1,0:T(8,128)S(1)} %get-tuple-element.71) | copy-start | bytes 2359300
  209.4 85.3 %copy-start.48 = (s32[100]{0:T(128)S(1)}, s32[100]{0:T(128)}, u32[]{:S(2)}) copy-start(s32[100]{0:T(128)} %param.14) | copy-start | bytes 1204
  249.6 63.6 %collective-permute-start.6 = (f32[3,8,2,384]{3,2,1,0:T(2,128)S(1)}, f32[3,8,2,384]{3,2,1,0:T(2,128)S(1)}, u32[]{:S(2)}, u32[]{:S(2)}) collective-permute-start(f32[3,8,2,384]{3,2,1,0:T(2,128)S(1)} %get-tuple-element.105), channel_id=1, source_target_pairs={{1,0},{2,1},{3,2},{4,3},{5,4},{6,5},{7,6},{0,7},{9,8},{10,9},{11,1... | collective-permute-start | bytes 221192 | tf_op jit(solution)/shard_map/ppermute | solution.py:35
  250.0 63.2 %collective-permute-start.7 = (f32[3,8,2,384]{3,2,1,0:T(2,128)S(1)}, f32[3,8,2,384]{3,2,1,0:T(2,128)S(1)}, u32[]{:S(2)}, u32[]{:S(2)}) collective-permute-start(f32[3,8,2,384]{3,2,1,0:T(2,128)S(1)} %get-tuple-element.104), channel_id=1, source_target_pairs={{0,1},{1,2},{2,3},{3,4},{4,5},{5,6},{6,7},{7,0},{8,9},{9,10},{10,1... | collective-permute-start | bytes 221192 | tf_op jit(solution)/shard_map/ppermute | solution.py:34
  251.4 61.9 %collective-permute-start.4 = (f32[3,2,64,384]{3,2,1,0:T(8,128)}, f32[3,2,64,384]{3,2,1,0:T(8,128)}, u32[]{:S(2)}, u32[]{:S(2)}) collective-permute-start(f32[3,2,64,384]{3,2,1,0:T(8,128)} %get-tuple-element.103), channel_id=1, source_target_pairs={{8,0},{16,8},{24,16},{32,24},{40,32},{48,40},{56,48},{64,56},{72,6... | collective-permute-start | bytes 1769480 | tf_op jit(solution)/shard_map/ppermute | solution.py:35
  253.7 59.6 %collective-permute-start.5 = (f32[3,2,64,384]{3,2,1,0:T(8,128)}, f32[3,2,64,384]{3,2,1,0:T(8,128)}, u32[]{:S(2)}, u32[]{:S(2)}) collective-permute-start(f32[3,2,64,384]{3,2,1,0:T(8,128)} %get-tuple-element.102), channel_id=1, source_target_pairs={{0,8},{8,16},{16,24},{24,32},{32,40},{40,48},{48,56},{56,64},{64,7... | collective-permute-start | bytes 1769480 | tf_op jit(solution)/shard_map/ppermute | solution.py:34
  346.4 101.3 %copy-start.36 = (f32[2,384]{1,0:T(2,128)S(1)}, f32[2,384]{1,0:T(2,128)}, u32[]{:S(2)}) copy-start(f32[2,384]{1,0:T(2,128)} %param.9) | copy-start | bytes 9220
  346.5 101.5 %copy-start.4 = (f32[1,8,64,384]{3,2,1,0:T(8,128)S(1)}, f32[1,8,64,384]{3,2,1,0:T(8,128)}, u32[]{:S(2)}) copy-start(f32[1,8,64,384]{3,2,1,0:T(8,128)} %copy-done.3) | copy-start | bytes 2359300
  346.5 101.5 %copy-start.6 = (f32[1,8,64,384]{3,2,1,0:T(8,128)S(1)}, f32[1,8,64,384]{3,2,1,0:T(8,128)}, u32[]{:S(2)}) copy-start(f32[1,8,64,384]{3,2,1,0:T(8,128)} %copy-done.5) | copy-start | bytes 2359300
  386.2 61.7 %collective-permute-start.10 = (f32[3,8,2,384]{3,2,1,0:T(2,128)S(1)}, f32[3,8,2,384]{3,2,1,0:T(2,128)S(1)}, u32[]{:S(2)}, u32[]{:S(2)}) collective-permute-start(f32[3,8,2,384]{3,2,1,0:T(2,128)S(1)} %get-tuple-element.97), channel_id=1, source_target_pairs={{1,0},{2,1},{3,2},{4,3},{5,4},{6,5},{7,6},{0,7},{9,8},{10,9},{11,1... | collective-permute-start | bytes 221192 | tf_op jit(solution)/shard_map/ppermute | solution.py:35
  386.5 61.4 %collective-permute-start.11 = (f32[3,8,2,384]{3,2,1,0:T(2,128)S(1)}, f32[3,8,2,384]{3,2,1,0:T(2,128)S(1)}, u32[]{:S(2)}, u32[]{:S(2)}) collective-permute-start(f32[3,8,2,384]{3,2,1,0:T(2,128)S(1)} %get-tuple-element.96), channel_id=1, source_target_pairs={{0,1},{1,2},{2,3},{3,4},{4,5},{5,6},{6,7},{7,0},{8,9},{9,10},{10,1... | collective-permute-start | bytes 221192 | tf_op jit(solution)/shard_map/ppermute | solution.py:34
  387.9 60.0 %collective-permute-start.8 = (f32[3,2,64,384]{3,2,1,0:T(8,128)}, f32[3,2,64,384]{3,2,1,0:T(8,128)S(1)}, u32[]{:S(2)}, u32[]{:S(2)}) collective-permute-start(f32[3,2,64,384]{3,2,1,0:T(8,128)} %get-tuple-element.95), channel_id=1, source_target_pairs={{8,0},{16,8},{24,16},{32,24},{40,32},{48,40},{56,48},{64,56},{72,6... | collective-permute-start | bytes 1769480 | tf_op jit(solution)/shard_map/ppermute | solution.py:35
  389.5 58.5 %collective-permute-start.9 = (f32[3,2,64,384]{3,2,1,0:T(8,128)}, f32[3,2,64,384]{3,2,1,0:T(8,128)}, u32[]{:S(2)}, u32[]{:S(2)}) collective-permute-start(f32[3,2,64,384]{3,2,1,0:T(8,128)} %get-tuple-element.94), channel_id=1, source_target_pairs={{0,8},{8,16},{16,24},{24,32},{32,40},{40,48},{48,56},{56,64},{64,7... | collective-permute-start | bytes 1769480 | tf_op jit(solution)/shard_map/ppermute | solution.py:34
  477.4 105.4 %copy-start.61 = (f32[1,4]{1,0:T(1,128)S(1)}, f32[1,4]{1,0:T(1,128)}, u32[]{:S(2)}) copy-start(f32[1,4]{1,0:T(1,128)} %param.15) | copy-start | bytes 52
  477.4 105.4 %copy-start.63 = (s32[100]{0:T(128)S(1)}, s32[100]{0:T(128)}, u32[]{:S(2)}) copy-start(s32[100]{0:T(128)} %copy-done.62) | copy-start | bytes 1204
  477.4 105.4 %copy-start.65 = (pred[100]{0:T(512)(128)(4,1)S(1)}, pred[100]{0:T(512)(128)(4,1)}, u32[]{:S(2)}) copy-start(pred[100]{0:T(512)(128)(4,1)} %copy-done.64) | copy-start | bytes 304
  477.4 105.4 %copy-start.66 = (f32[4]{0:T(128)S(1)}, f32[4]{0:T(128)}, u32[]{:S(2)}) copy-start(f32[4]{0:T(128)} %convert_reduce_fusion.1) | copy-start | bytes 52
  477.5 106.9 %copy-start.33 = (f32[4,384]{1,0:T(4,128)S(1)}, f32[4,384]{1,0:T(4,128)}, u32[]{:S(2)}) copy-start(f32[4,384]{1,0:T(4,128)} %copy-done.32) | copy-start | bytes 18436
  477.5 106.9 %copy-start.42 = (f32[1,384]{1,0:T(1,128)S(1)}, f32[1,384]{1,0:T(1,128)}, u32[]{:S(2)}) copy-start(f32[1,384]{1,0:T(1,128)} %fusion.105) | copy-start | bytes 4612
  477.5 106.9 %copy-start.43 = (f32[1,384]{1,0:T(1,128)S(1)}, f32[1,384]{1,0:T(1,128)}, u32[]{:S(2)}) copy-start(f32[1,384]{1,0:T(1,128)} %fusion.104) | copy-start | bytes 4612
  479.3 105.7 %collective-permute-start.14 = (f32[3,8,2,384]{3,2,1,0:T(2,128)S(1)}, f32[3,8,2,384]{3,2,1,0:T(2,128)S(1)}, u32[]{:S(2)}, u32[]{:S(2)}) collective-permute-start(f32[3,8,2,384]{3,2,1,0:T(2,128)S(1)} %get-tuple-element.88), channel_id=1, source_target_pairs={{1,0},{2,1},{3,2},{4,3},{5,4},{6,5},{7,6},{0,7},{9,8},{10,9},{11,1... | collective-permute-start | bytes 221192 | tf_op jit(solution)/shard_map/ppermute | solution.py:35
  479.6 105.4 %collective-permute-start.15 = (f32[3,8,2,384]{3,2,1,0:T(2,128)S(1)}, f32[3,8,2,384]{3,2,1,0:T(2,128)S(1)}, u32[]{:S(2)}, u32[]{:S(2)}) collective-permute-start(f32[3,8,2,384]{3,2,1,0:T(2,128)S(1)} %get-tuple-element.87), channel_id=1, source_target_pairs={{0,1},{1,2},{2,3},{3,4},{4,5},{5,6},{6,7},{7,0},{8,9},{9,10},{10,1... | collective-permute-start | bytes 221192 | tf_op jit(solution)/shard_map/ppermute | solution.py:34
  481.1 104.0 %collective-permute-start.12 = (f32[3,2,64,384]{3,2,1,0:T(8,128)}, f32[3,2,64,384]{3,2,1,0:T(8,128)S(1)}, u32[]{:S(2)}, u32[]{:S(2)}) collective-permute-start(f32[3,2,64,384]{3,2,1,0:T(8,128)} %get-tuple-element.86), channel_id=1, source_target_pairs={{8,0},{16,8},{24,16},{32,24},{40,32},{48,40},{56,48},{64,56},{72,6... | collective-permute-start | bytes 1769480 | tf_op jit(solution)/shard_map/ppermute | solution.py:35
  481.1 104.0 %collective-permute-start.13 = (f32[3,2,64,384]{3,2,1,0:T(8,128)}, f32[3,2,64,384]{3,2,1,0:T(8,128)}, u32[]{:S(2)}, u32[]{:S(2)}) collective-permute-start(f32[3,2,64,384]{3,2,1,0:T(8,128)} %get-tuple-element.85), channel_id=1, source_target_pairs={{0,8},{8,16},{16,24},{24,32},{32,40},{40,48},{48,56},{56,64},{64,7... | collective-permute-start | bytes 1769480 | tf_op jit(solution)/shard_map/ppermute | solution.py:34
  (55 other events, 1296.4 us)
